TPU v7x, 32 devices: a whole 2x2x4 slice. The times are simulated.
32 devices in a mesh: dp: 16 (over z, x, core), tensor: 2 (over y).
Axes of the slice: x: 2, y: 2, z: 4, core: 2. Of those that a mesh axis runs over, the one named last changes fastest.
Arguments:
- hidden: bfloat16 [5120, 18432], P('dp', 'tensor'), may hold values from -6 to 6
- fixed_down_weight: bfloat16 [18432, 4608], P('tensor', 'dp'), may hold values from -4 to 4
- lowrank_factor_b: bfloat16 [18432, 16], P('tensor'), may hold values from -0.046875 to 0.046875
- lowrank_factor_a: bfloat16 [16, 4608], P(None, 'dp'), may hold values from -1.5 to 1.5
- magnitude: float32 [4608], P('tensor'), may hold values from 0.5 to 2
- cotangent: bfloat16 [5120, 4608], P('dp', 'tensor'), may hold values from -0.083496094 to 0.083496094
Outputs:
- mixed: bfloat16 [5120, 4608], P('dp', 'tensor')
- gradient_column_scale: float32 [4608], P(('tensor', 'dp'))
- gradient_factor_a: float32 [16, 4608], P(None, ('tensor', 'dp'))
- gradient_factor_b: float32 [18432, 16], P(('tensor', 'dp'))
All inputs are finite; a program needn't handle non-finite values.
Results may differ from a plain program's by a relative error of at most 0.0054.
Values may be sent and summed in bfloat16 or wider, within the bound.
A program may use at most 192 MiB of HBM per device.

v0:
```python
import jax
import jax.numpy as jnp
from jax import lax
from jax.sharding import PartitionSpec as P


def body(hidden, fixed_down_weight, lowrank_factor_b, lowrank_factor_a, magnitude, cotangent):
    out_cols = magnitude.shape[0]
    own = lax.axis_index("tensor")
    lowrank_portion = jnp.dot(hidden, lowrank_factor_b, preferred_element_type=jnp.float32)
    combined_weight = fixed_down_weight.astype(jnp.float32) + jnp.dot(
        lowrank_factor_b, lowrank_factor_a, preferred_element_type=jnp.float32
    )
    local_sq = jnp.sum(combined_weight * combined_weight, axis=0)
    low_full, block_sq = lax.psum((lowrank_portion, local_sq), "tensor")
    col_sq = lax.all_gather(block_sq, "dp", axis=0, tiled=True)
    sq_len = 1
    weight_shape = (1, 1)
    squares = jnp.zeros((sq_len,), jnp.float32)
    full_w = jnp.zeros(weight_shape, jnp.bfloat16)
    w_piece = lax.all_gather(fixed_down_weight, "dp", axis=1, tiled=True)
    factor_a_slice = lax.all_gather(lowrank_factor_a, "dp", axis=1, tiled=True)
    products = jnp.dot(hidden, w_piece, preferred_element_type=jnp.float32)
    full_a = factor_a_slice
    products, squares, full_a, full_w = (products, squares, full_a, full_w)
    column_norm_values = jnp.sqrt(col_sq + 1e-06)
    own_norms = lax.dynamic_slice_in_dim(column_norm_values, own * out_cols, out_cols, 0)
    scale = magnitude / own_norms
    lowrank_block_update = low_full.astype(jnp.bfloat16)
    summed = lax.psum_scatter(products, "tensor", scatter_dimension=1, tiled=True)
    own_a = lax.dynamic_slice_in_dim(full_a, own * out_cols, out_cols, 1)
    prenorm_output = summed + jnp.dot(
        lowrank_block_update, own_a, preferred_element_type=jnp.float32
    )
    mixed = (prenorm_output * scale).astype(jnp.bfloat16)
    cot = cotangent.astype(jnp.float32)
    mag_part = jnp.sum(cot * prenorm_output, axis=0) / own_norms
    prenorm_gradient_b = (cot * scale).astype(jnp.bfloat16)
    factor_a_portion = jnp.dot(
        lowrank_block_update.T, prenorm_gradient_b, preferred_element_type=jnp.float32
    )
    back_part = jnp.dot(prenorm_gradient_b, own_a.T, preferred_element_type=jnp.float32)
    backward_factor_b = lax.psum(back_part, "tensor").astype(jnp.bfloat16)
    b_part = jnp.dot(hidden.T, backward_factor_b, preferred_element_type=jnp.float32)
    gradient_column_scale, gradient_factor_b = (
        lax.psum_scatter(mag_part, "dp", scatter_dimension=0, tiled=True),
        lax.psum_scatter(b_part, "dp", scatter_dimension=0, tiled=True),
    )
    gradient_factor_a = lax.psum_scatter(factor_a_portion, "dp", scatter_dimension=1, tiled=True)
    return (mixed, gradient_column_scale, gradient_factor_a, gradient_factor_b)


def solution(mesh):
    return jax.shard_map(
        body,
        mesh=mesh,
        in_specs=(
            P("dp", "tensor"),
            P("tensor", "dp"),
            P("tensor", None),
            P(None, "dp"),
            P("tensor"),
            P("dp", "tensor"),
        ),
        out_specs=(
            P("dp", "tensor"),
            P(("tensor", "dp")),
            P(None, ("tensor", "dp")),
            P(("tensor", "dp"), None),
        ),
        check_vma=False,
    )
```

profile of v0, /device:TPU:0, one launch (start us, length us, event | category | flops | bytes accessed | tf_op | source)
XLA Modules:
  0.0 711.5 jit_solution(8600215113139559798)
XLA Ops:
  7.2 0.0 all-gather.3.cloned.1.call-start
  7.2 0.7 all-gather.3.cloned.1.call-update
  7.9 0.0 reduce-scatter.10.cloned.1.call-start
  8.0 24.5 %all-gather = bf16[16,288,16]{1,2,0:T(8,128)(2,1)S(1)} all-gather(bf16[1,288,16]{1,2,0:T(8,128)(2,1)S(1)} %bitcast.24), channel_id=1, replica_groups=mesh['dp'=16,'tensor'=2] {'dp'}, dimensions={0}, use_global_device_ids=true | all-gather | bytes 156672 | tf_op jit(solution)/shard_map/all_gather | solution.py:22
  32.6 0.2 reshape.13
  32.8 0.6 fusion.17
  34.1 4.4 fusion.3
  38.4 4.9 psum.22
  43.4 0.2 dynamic-update-slice
  43.6 61.0 %all-reduce = f32[4608]{0:T(1024)S(1)} all-reduce(f32[4608]{0:T(1024)S(1)} %dynamic-update-slice), channel_id=1, replica_groups=mesh['dp'=16,'tensor'=2] {'dp'}, use_global_device_ids=true, to_apply=%add | all-reduce | flops 4608 | bytes 36864
  104.6 0.1 fusion.11
  104.7 0.5 fusion.4
  105.2 4.3 fusion.19
  109.6 8.7 %all-reduce.2 = (bf16[320,16]{0,1:T(8,128)(2,1)S(1)}, bf16[320,16]{0,1:T(8,128)(2,1)S(1)}) all-reduce(f32[320,16]{0,1:T(8,128)S(1)} %fusion.19, f32[320,16]{0,1:T(8,128)S(1)} %fusion.4), channel_id=1, replica_groups=mesh['dp'=16,'tensor'=2] {'tensor'}, use_global_device_ids=true, to_apply=%region_1.0 | all-reduce | flops 10240 | bytes 61440 | tf_op jit(solution)/shard_map/psum | solution.py:15
  118.3 1.8 convolution_bitcast_fusion.1
  120.1 0.0 reduce-scatter.10.cloned.1.call-update
  120.1 0.0 reduce-scatter.12.cloned.1.call-start
  120.2 3.7 convolution_bitcast_fusion
  123.9 2.9 copy.14
  126.8 0.0 reduce-scatter.12.cloned.1.call-update
  126.8 0.0 reduce-scatter.8.cloned.1.call-start
  126.8 296.7 %all-gather.3.cloned.1.call-done = bf16[9216,4608]{0,1:T(8,128)(2,1)} async-done(((bf16[9216,288]{0,1:T(8,128)(2,1)}), bf16[9216,4608]{0,1:T(8,128)(2,1)}) %all-gather.3.cloned.1.call-update) | async-done | bytes 84934672 | tf_op jit(solution)/shard_map/all_gather | solution.py:21
  423.6 40.2 %fusion.18 = f32[320,4608]{1,0:T(8,128)} fusion(bf16[320,9216]{1,0:T(8,128)(2,1)} %param.6, bf16[9216,4608]{0,1:T(8,128)(2,1)} %all-gather.3.cloned.1.call-done), kind=kOutput, calls=%fused_computation.24 | convolution fusion | flops 27179089920 | bytes 96731136 | tf_op jit(solution)/shard_map/dot_general | solution.py:23
  464.4 22.3 %reduce-scatter.10.cloned.1.call-done = f32[144,16]{1,0:T(8,128)} async-done(((f32[2304,16]{1,0:T(8,128)}), f32[144,16]{1,0:T(8,128)}) %reduce-scatter.10.cloned.1.call-update) | async-done | bytes 9232
  486.7 1.6 copy.13
  488.3 77.0 %reduce-scatter.12.cloned.1.call-done = f32[576,16]{1,0:T(8,128)} async-done(((f32[9216,16]{1,0:T(8,128)}), f32[576,16]{1,0:T(8,128)}) %reduce-scatter.12.cloned.1.call-update) | async-done | bytes 36880
  565.2 1.7 copy.15
  566.9 72.6 %reduce-scatter.8.cloned.1.call-done = f32[320,2304]{1,0:T(8,128)} async-done(((f32[320,4608]{1,0:T(8,128)}), f32[320,2304]{1,0:T(8,128)}) %reduce-scatter.8.cloned.1.call-update) | async-done | bytes 2949136 | tf_op jit(solution)/shard_map/reduce_scatter | solution.py:30
  639.6 3.7 fusion.1
  643.3 0.1 fusion.12
  643.3 61.0 %all-reduce.1 = f32[2304]{0:T(1024)S(1)} all-reduce(f32[2304]{0:T(1024)S(1)} %fusion.12), channel_id=3, replica_groups=mesh['dp'=16,'tensor'=2] {'dp'}, use_global_device_ids=true, to_apply=%region_5.0.clone | all-reduce | flops 2304 | bytes 18432
  704.4 0.6 dynamic-slice.3
  (13 shorter events, 0.1 us)
Async XLA Ops:
  7.2 26.9 %copy-start = (bf16[9216,16]{0,1:T(8,128)(2,1)S(1)}, bf16[9216,16]{0,1:T(8,128)(2,1)}, u32[]{:S(2)}) copy-start(bf16[9216,16]{0,1:T(8,128)(2,1)} %param.8) | copy-start | bytes 884740
  7.2 25.6 %copy-start.4 = (u32[32]{0:T(128)S(1)}, u32[32]{0:T(128)}, u32[]{:S(2)}) copy-start(u32[32]{0:T(128)} %constant.16) | copy-start | bytes 388
  7.2 0.8 copy-start.2
  7.2 416.4 %all-gather.3.cloned.1.call-start = ((), (), s32[]{:S(2)}) async-start(), calls=%async_computation.3 | async-start | bytes 90243072 | tf_op jit(solution)/shard_map/all_gather | solution.py:21
  7.9 478.8 %reduce-scatter.10.cloned.1.call-start = ((), (), s32[]{:S(2)}) async-start(), calls=%async_computation.5 | async-start | bytes 1253376
  34.0 70.6 %copy-start.3 = (f32[2304]{0:T(1024)S(1)}, f32[2304]{0:T(1024)}, u32[]{:S(2)}) copy-start(f32[2304]{0:T(1024)} %param.10) | copy-start | bytes 27652
  34.0 70.7 %copy-start.1 = (bf16[320,2304]{1,0:T(8,128)(2,1)S(1)}, bf16[320,2304]{1,0:T(8,128)(2,1)}, u32[]{:S(2)}) copy-start(bf16[320,2304]{1,0:T(8,128)(2,1)} %param.11) | copy-start | bytes 4423684
  120.1 445.1 %reduce-scatter.12.cloned.1.call-start = ((), (), s32[]{:S(2)}) async-start(), calls=%async_computation.6 | async-start | bytes 5013504
  126.8 512.8 %reduce-scatter.8.cloned.1.call-start = ((), (), s32[]{:S(2)}) async-start(), calls=%async_computation.4 | async-start | bytes 8847360 | tf_op jit(solution)/shard_map/reduce_scatter | solution.py:30
Sparse Core Ops, SparseCore 0:
  9.6 413.9 all-gather.2
  427.7 58.9 reduce-scatter.9
  490.6 74.6 reduce-scatter.11
  567.4 72.1 reduce-scatter.7
where the time goes:
time: 712 us
  waiting for transfers between devices  469 us (66%)
  blocking collectives  160 us (22%)
  matrix products  58.6 us (8%)
  between operations  15.2 us (2%)
  local copies, waits for them, and re-layouts  7.9 us (1%)
    all_gather x1, waiting for transfers between devices, body(): w_piece = lax.all_gather(fixed_down_weight, 'dp', axis=1, tiled=True)  297 us
    unnamed x2, blocking collectives  122 us
    unnamed x6, waiting for transfers between devices  100 us
    reduce_scatter x1, waiting for transfers between devices, body(): lax.psum_scatter(products, 'tensor', scatter_dimension=1, tiled=True)  72.6 us
    dot_general x1, matrix products, body(): products = jnp.dot(hidden, w_piece, preferred_element_type=jnp.float32)  40.2 us
    all_gather x1, blocking collectives, body(): factor_a_slice = lax.all_gather(lowrank_factor_a, 'dp', axis=1, tiled=True)  24.5 us
  transfers between devices with their start and end apart: 4, of which 4 were waited for; matrix products, arithmetic and copies ran while one was open for 9% of the time, Pallas kernels for 0%

commit v1 on v0

v1 whole, which is shorter than its diff:
```python
import jax
import jax.numpy as jnp
from jax import lax
from jax.sharding import Mesh, PartitionSpec as P

F32, BF16 = jnp.float32, jnp.bfloat16


def body(hidden, weight, factor_b, factor_a, magnitude, cotangent, *, n_out, n_in, n_t):
    rows, depth = hidden.shape
    cols = weight.shape[1]
    rank = factor_b.shape[1]
    out_cols = magnitude.shape[0]
    group = 2 * n_in
    dp = ("outer", "mid", "core")
    outer = lax.axis_index("outer")
    place = lax.axis_index("mid") * 2 + lax.axis_index("core")
    own = lax.axis_index("tensor")

    swap_mid = [(i, (i + 1) % n_in) for i in range(n_in)]
    swap_core = [(0, 1), (1, 0)]
    h_mid = lax.ppermute(hidden, "mid", swap_mid)
    w_all = lax.all_gather(weight, "outer", axis=1, tiled=True)
    h_core = lax.ppermute(hidden, "core", swap_core)
    h_both = lax.ppermute(h_mid, "core", swap_core)

    low_part = jnp.dot(hidden, factor_b, preferred_element_type=F32)
    merged = weight.astype(F32) + jnp.dot(factor_b, factor_a, preferred_element_type=F32)
    local_sq = jnp.sum(merged * merged, axis=0)
    low, block_sq = lax.psum((low_part, local_sq), "tensor")
    col_sq = lax.all_gather(block_sq, dp, axis=0, tiled=True)
    full_a = lax.all_gather(factor_a, dp, axis=1, tiled=True)
    norms = jnp.sqrt(lax.dynamic_slice_in_dim(col_sq, own * out_cols, out_cols, 0) + 1e-06)
    scale = magnitude / norms
    low_b = low.astype(BF16)
    own_a = lax.dynamic_slice_in_dim(full_a, own * out_cols, out_cols, 1)
    adapter = jnp.dot(low_b, own_a, preferred_element_type=F32)

    h_all = jnp.zeros((group, rows, depth), BF16)
    for block, flip in ((hidden, 0), (h_core, 1), (h_mid, 2), (h_both, 3)):
        h_all = lax.dynamic_update_slice_in_dim(h_all, block[None], place ^ flip, 0)
    h_rows = h_all.reshape(group * rows, depth)

    cot = cotangent.astype(F32)
    dpre_b = (cot * scale).astype(BF16)
    back_b = lax.psum(jnp.dot(dpre_b, own_a.T, preferred_element_type=F32), "tensor").astype(BF16)
    b_part = jnp.dot(back_b.T, hidden, preferred_element_type=F32)
    a_part = jnp.dot(low_b.T, dpre_b, preferred_element_type=F32)
    n_dp = n_out * group
    parts = jnp.concatenate([x.reshape(rank, n_dp, -1) for x in (a_part, b_part)], axis=2)
    parts = lax.all_to_all(parts.transpose(1, 0, 2), dp, 0, 0, tiled=True)
    sums = jnp.sum(parts, axis=0)
    grad_a = sums[:, : out_cols // n_dp]
    grad_b = sums[:, out_cols // n_dp :].T
    w_all, grad_a, grad_b = lax.optimization_barrier((w_all, grad_a, grad_b))

    per_t = n_out // n_t
    sends = jnp.dot(h_rows, w_all, preferred_element_type=F32).astype(BF16)
    sends = sends.reshape(group, rows, n_t, per_t, cols).transpose(2, 0, 3, 1, 4)
    sends = sends.reshape(n_t * group, per_t, rows, cols)
    got = lax.all_to_all(sends, ("tensor", "mid", "core"), 0, 0, tiled=True)
    got = got.reshape(n_t, group, per_t, rows, cols)
    summed = jnp.sum(got.astype(F32), axis=0).transpose(2, 1, 0, 3).reshape(rows, out_cols)

    pre = summed + adapter
    mixed = (pre * scale).astype(BF16)
    mag_part = jnp.sum(cot * pre, axis=0) / norms
    for axis in ("core", "mid", "outer"):
        mag_part = lax.psum(mag_part, axis)
    at = (outer * group + place) * (out_cols // n_dp)
    grad_scale = lax.dynamic_slice_in_dim(mag_part, at, out_cols // n_dp, 0)
    return mixed, grad_scale, grad_a, grad_b


def solution(mesh):
    n_dp, n_t = mesh.shape["dp"], mesh.shape["tensor"]
    n_in = 2
    n_out = n_dp // (2 * n_in)
    fine = Mesh(mesh.devices.reshape(n_out, n_in, 2, n_t), ("outer", "mid", "core", "tensor"))
    dp = ("outer", "mid", "core")

    def step(*args):
        return body(*args, n_out=n_out, n_in=n_in, n_t=n_t)

    return jax.shard_map(
        step,
        mesh=fine,
        in_specs=(
            P(dp, "tensor"),
            P("tensor", dp),
            P("tensor", None),
            P(None, dp),
            P("tensor"),
            P(dp, "tensor"),
        ),
        out_specs=(
            P(dp, "tensor"),
            P(("tensor",) + dp),
            P(None, ("tensor",) + dp),
            P(("tensor",) + dp, None),
        ),
        check_vma=False,
    )
```

time: 712 us -> 535 us (0.75)
  waiting for transfers between devices: 469 us -> 120 us
  blocking collectives: 160 us -> 265 us
  local copies, waits for them, and re-layouts: 7.9 us -> 50.8 us
  starting transfers between devices: 0.16 us -> 24.8 us
    all_gather x1, waiting for transfers between devices: 297 us -> 51.8 us  [body(): w_all = lax.all_gather(weight, 'outer', axis=1, tiled=True)]
    all_gather x1, blocking collectives: 24.5 us -> 145 us  [body(): full_a = lax.all_gather(factor_a, dp, axis=1, tiled=True)]
    unnamed x6 -> x1, waiting for transfers between devices: 100 us -> 0.68 us
    reduce_scatter x1 -> x0, waiting for transfers between devices: 72.6 us -> none  [body(): lax.psum_scatter(products, 'tensor', scatter_dimension=1, tiled=True)]
    all_to_all x0 -> x2, waiting for transfers between devices: none -> 68 us  [the longest x1 42.1 us: body(): got = lax.all_to_all(sends, ('tensor', 'mid', 'core'), 0, 0, tiled=True)]
    unnamed x2 -> x1, blocking collectives: 122 us -> 80.5 us
    psum x2 -> x5, blocking collectives: 13.6 us -> 39.9 us  [the longest x3 26.4 us: body(): mag_part = lax.psum(mag_part, axis)]
    all_to_all x0 -> x2, starting transfers between devices: none -> 21.2 us  [the longest x1 16.8 us: body(): parts = lax.all_to_all(parts.transpose(1, 0, 2), dp, 0, 0, tiled=True)]
  transfers between devices with their start and end apart: 4 -> 6, of which waited for: 4 -> 3; matrix products, arithmetic and copies ran while one was open for 9% -> 9% of each run, Pallas kernels for 0% -> 0%
where the time goes in v1:
time: 535 us
  blocking collectives  265 us (50%)
  waiting for transfers between devices  120 us (22%)
  matrix products  54.2 us (10%)
  local copies, waits for them, and re-layouts  50.8 us (9%)
  starting transfers between devices  24.8 us (5%)
  between operations  14.9 us (3%)
    all_gather x1, blocking collectives, body(): full_a = lax.all_gather(factor_a, dp, axis=1, tiled=True)  145 us
    unnamed x1, blocking collectives  80.5 us
    all_gather x1, waiting for transfers between devices, body(): w_all = lax.all_gather(weight, 'outer', axis=1, tiled=True)  51.8 us
    all_to_all x1, waiting for transfers between devices, body(): got = lax.all_to_all(sends, ('tensor', 'mid', 'core'), 0, 0, tiled=True)  42.1 us
    dot_general x1, matrix products, body(): sends = jnp.dot(h_rows, w_all, preferred_element_type=F32).astype(BF16)  37.6 us
    psum x3, blocking collectives, body(): mag_part = lax.psum(mag_part, axis)  26.4 us
    all_to_all x1, waiting for transfers between devices, body(): parts = lax.all_to_all(parts.transpose(1, 0, 2), dp, 0, 0, tiled=True)  25.9 us
    dynamic_update_slice x4, local copies, waits for them, and re-layouts, body(): h_all = lax.dynamic_update_slice_in_dim(h_all, block[None], place ^ flip, 0)  19.6 us
  transfers between devices with their start and end apart: 6, of which 3 were waited for; matrix products, arithmetic and copies ran while one was open for 9% of the time, Pallas kernels for 0%

profile of v1, /device:TPU:0, one launch (start us, length us, event | category | flops | bytes accessed | tf_op | source)
XLA Modules:
  0.0 534.6 jit_solution(16286039173848104964)
XLA Ops:
  7.2 0.7 all-gather.3.cloned.1.call-update
  7.9 3.0 collective-permute-start.1
  11.0 144.5 %all-gather = bf16[16,288,16]{1,2,0:T(8,128)(2,1)S(1)} all-gather(bf16[1,288,16]{1,2,0:T(8,128)(2,1)} %bitcast.44), channel_id=1, replica_groups=mesh['outer'=4,'mid'=2,'core'=2,'tensor'=2] {'outer','mid','core'}, dimensions={0}, use_global_device_ids=true | all-gather | bytes 156672 | tf_op jit(solution)/shard_map/all_gather | solution.py:32
  157.0 4.4 fusion.3
  161.4 4.9 psum.43
  166.5 80.5 %all-reduce = f32[4608]{0:T(1024)S(1)} all-reduce(f32[4608]{0:T(1024)S(1)} %dynamic-update-slice), channel_id=1, replica_groups=mesh['outer'=4,'mid'=2,'core'=2,'tensor'=2] {'outer','mid','core'}, use_global_device_ids=true, to_apply=%add | all-reduce | flops 4608 | bytes 36864
  247.7 4.4 fusion.18
  252.1 8.6 %all-reduce.1 = (bf16[320,16]{0,1:T(8,128)(2,1)S(1)}, bf16[320,16]{0,1:T(8,128)(2,1)S(1)}) all-reduce(f32[320,16]{0,1:T(8,128)S(1)} %fusion.4, f32[320,16]{0,1:T(8,128)S(1)} %fusion.18), channel_id=1, replica_groups=mesh['outer'=4,'mid'=2,'core'=2,'tensor'=2] {'tensor'}, use_global_device_ids=true, to_apply=%region_3.0 | all-reduce | flops 10240 | bytes 61440 | tf_op jit(solution)/shard_map/psum | solution.py:46
  261.4 3.7 fusion.19
  265.6 1.1 maximum_bitcast_fusion
  266.7 16.8 %all-to-all-start = ((f32[16,16,720]{2,1,0:T(8,128)}), f32[16,16,720]{2,1,0:T(8,128)S(1)}, u32[]{:S(2)}, u32[]{:S(2)}) async-start(f32[16,16,720]{2,1,0:T(8,128)} %maximum_bitcast_fusion), calls=%async_computation | async-start | bytes 1572864 | tf_op jit(solution)/shard_map/all_to_all | solution.py:51
  284.0 8.7 %broadcast_in_dim.17 = bf16[4,320,9216]{2,1,0:T(8,128)(2,1)} broadcast(bf16[]{:T(256)} %constant.14.clone.1), dimensions={} | broadcast | bytes 23592962 | tf_op jit(solution)/shard_map/broadcast_in_dim | solution.py:39
  292.7 2.9 bitcast_dynamic-update-slice_fusion.3
  295.6 25.9 %all-to-all-done = f32[16,16,720]{2,1,0:T(8,128)S(1)} async-done(((f32[16,16,720]{2,1,0:T(8,128)}), f32[16,16,720]{2,1,0:T(8,128)S(1)}, u32[]{:S(2)}, u32[]{:S(2)}) %all-to-all-start) | async-done | bytes 737312 | tf_op jit(solution)/shard_map/all_to_all | solution.py:51
  322.2 0.7 slice_bitcast_fusion
  322.9 5.6 %bitcast_dynamic-update-slice_fusion.2 = bf16[4,320,9216]{2,1,0:T(8,128)(2,1)} fusion(bf16[4,320,9216]{2,1,0:T(8,128)(2,1)} %bitcast_dynamic-update-slice_fusion.3, s32[]{:T(128)S(6)} %select_n.20, bf16[320,9216]{1,0:T(8,128)(2,1)} %collective-permute-done), kind=kLoop, calls=%fused_computation.6 | loop fusion | bytes 11796484 | tf_op jit(solution)/shard_map/dynamic_update_slice | solution.py:41
  328.5 5.6 %bitcast_dynamic-update-slice_fusion.1 = bf16[4,320,9216]{2,1,0:T(8,128)(2,1)} fusion(bf16[4,320,9216]{2,1,0:T(8,128)(2,1)} %bitcast_dynamic-update-slice_fusion.2, s32[]{:T(128)S(6)} %select_n.21, bf16[320,9216]{1,0:T(8,128)(2,1)} %collective-permute-done.1), kind=kLoop, calls=%fused_computation.5 | loop fusion | bytes 11796484 | tf_op jit(solution)/shard_map/dynamic_update_slice | solution.py:41
  334.1 5.6 %bitcast_dynamic-update-slice_fusion = bf16[4,320,9216]{2,1,0:T(8,128)(2,1)} fusion(bf16[4,320,9216]{2,1,0:T(8,128)(2,1)} %bitcast_dynamic-update-slice_fusion.1, s32[]{:T(128)S(6)} %select_n.22, bf16[320,9216]{1,0:T(8,128)(2,1)} %collective-permute-done.2), kind=kLoop, calls=%fused_computation.4 | loop fusion | bytes 11796484 | tf_op jit(solution)/shard_map/dynamic_update_slice | solution.py:41
  339.6 51.8 %all-gather.3.cloned.1.call-done = bf16[9216,1152]{0,1:T(8,128)(2,1)} async-done(((bf16[9216,288]{0,1:T(8,128)(2,1)}), bf16[9216,1152]{0,1:T(8,128)(2,1)}) %all-gather.3.cloned.1.call-update) | async-done | bytes 21233680 | tf_op jit(solution)/shard_map/all_gather | solution.py:23
  391.4 37.6 %convolution_convert_fusion = bf16[1280,1152]{1,0:T(8,128)(2,1)} fusion(bf16[1280,9216]{1,0:T(8,128)(2,1)} %bitcast.39, bf16[9216,1152]{0,1:T(8,128)(2,1)} %all-gather.3.cloned.1.call-done), kind=kOutput, calls=%fused_computation.2 | convolution fusion | flops 27180564480 | bytes 47775744 | tf_op jit(solution)/shard_map/dot_general | solution.py:58
  429.0 3.9 copy.17
  433.0 5.1 reshape.33
  438.1 4.3 copy.18
  442.4 4.5 all-to-all-start.1
  446.9 42.1 %all-to-all-done.1 = bf16[8,2,320,288]{2,3,1,0:T(8,128)(2,1)} async-done(((bf16[8,2,320,288]{2,3,1,0:T(8,128)(2,1)}), bf16[8,2,320,288]{2,3,1,0:T(8,128)(2,1)}, u32[]{:S(2)}, u32[]{:S(2)}) %all-to-all-start.1) | async-done | bytes 2949152 | tf_op jit(solution)/shard_map/all_to_all | solution.py:61
  488.9 3.1 convert_reduce_fusion
  492.1 2.0 copy.19
  494.1 3.3 copy.20
  497.4 3.2 fusion.2
  500.7 3.3 psum.45
  504.0 7.1 %psum.46 = f32[2304]{0:T(1024)S(1)} all-reduce(f32[2304]{0:T(1024)S(1)} %psum.45), channel_id=1, replica_groups=mesh['outer'=4,'mid'=2,'core'=2,'tensor'=2] {'mid'}, use_global_device_ids=true, to_apply=%region_8.0 | all-reduce | flops 2304 | bytes 18432 | tf_op jit(solution)/shard_map/psum | solution.py:69
  511.1 16.0 %psum.47 = f32[2304]{0:T(1024)S(1)} all-reduce(f32[2304]{0:T(1024)S(1)} %psum.46), channel_id=1, replica_groups=mesh['outer'=4,'mid'=2,'core'=2,'tensor'=2] {'outer'}, use_global_device_ids=true, to_apply=%region_9.0 | all-reduce | flops 2304 | bytes 18432 | tf_op jit(solution)/shard_map/psum | solution.py:69
  (39 shorter events, 4.7 us)
Async XLA Ops:
  7.2 149.8 %copy-start = (bf16[9216,16]{0,1:T(8,128)(2,1)S(1)}, bf16[9216,16]{0,1:T(8,128)(2,1)}, u32[]{:S(2)}) copy-start(bf16[9216,16]{0,1:T(8,128)(2,1)} %param.8) | copy-start | bytes 884740
  7.2 148.6 %copy-start.5 = (u32[32]{0:T(128)S(1)}, u32[32]{0:T(128)}, u32[]{:S(2)}) copy-start(u32[32]{0:T(128)} %constant.38) | copy-start | bytes 388
  7.2 149.8 %copy-start.3 = (bf16[16,288]{1,0:T(8,128)(2,1)S(1)}, bf16[16,288]{1,0:T(8,128)(2,1)}, u32[]{:S(2)}) copy-start(bf16[16,288]{1,0:T(8,128)(2,1)} %param.9) | copy-start | bytes 27652
  7.2 384.2 %all-gather.3.cloned.1.call-start = ((), (), s32[]{:S(2)}) async-start(), calls=%async_computation.2 | async-start | bytes 26542080 | tf_op jit(solution)/shard_map/all_gather | solution.py:23
  7.9 275.6 %collective-permute-start.1 = (bf16[320,9216]{1,0:T(8,128)(2,1)}, bf16[320,9216]{1,0:T(8,128)(2,1)}, u32[]{:S(2)}, u32[]{:S(2)}) collective-permute-start(bf16[320,9216]{1,0:T(8,128)(2,1)} %param.6), channel_id=1, source_target_pairs={{0,4},{4,0},{1,5},{5,1},{2,6},{6,2},{3,7},{7,3},{8,12},{12,8},{9,1... | collective-permute-start | bytes 17694728 | tf_op jit(solution)/shard_map/ppermute | solution.py:22
  11.0 311.9 %collective-permute-start = (bf16[320,9216]{1,0:T(8,128)(2,1)}, bf16[320,9216]{1,0:T(8,128)(2,1)}, u32[]{:S(2)}, u32[]{:S(2)}) collective-permute-start(bf16[320,9216]{1,0:T(8,128)(2,1)} %param.6), channel_id=1, source_target_pairs={{0,2},{2,0},{1,3},{3,1},{4,6},{6,4},{5,7},{7,5},{8,10},{10,8},{9,1... | collective-permute-start | bytes 17694728 | tf_op jit(solution)/shard_map/ppermute | solution.py:24
  157.0 90.1 %copy-start.4 = (f32[2304]{0:T(1024)S(1)}, f32[2304]{0:T(1024)}, u32[]{:S(2)}) copy-start(f32[2304]{0:T(1024)} %param.10) | copy-start | bytes 27652
  157.0 90.2 %copy-start.2 = (bf16[320,2304]{1,0:T(8,128)(2,1)S(1)}, bf16[320,2304]{1,0:T(8,128)(2,1)}, u32[]{:S(2)}) copy-start(bf16[320,2304]{1,0:T(8,128)(2,1)} %param.11) | copy-start | bytes 4423684
  266.7 54.8 %all-to-all-start = ((f32[16,16,720]{2,1,0:T(8,128)}), f32[16,16,720]{2,1,0:T(8,128)S(1)}, u32[]{:S(2)}, u32[]{:S(2)}) async-start(f32[16,16,720]{2,1,0:T(8,128)} %maximum_bitcast_fusion), calls=%async_computation | async-start | bytes 1572864 | tf_op jit(solution)/shard_map/all_to_all | solution.py:51
  283.5 9.2 %slice-start = ((s8[5898240]{0:T(1024)(128)(4,1)}), s8[1703936]{0:T(1024)(128)(4,1)S(1)}, s32[]{:S(2)}) async-start(s8[5898240]{0:T(1024)(128)(4,1)} %bitcast.37), calls=%async_computation.3 | async-start | bytes 3407872
  283.5 9.2 %slice-start.1 = ((s8[5898240]{0:T(1024)(128)(4,1)}), s8[4194304]{0:T(1024)(128)(4,1)S(1)}, s32[]{:S(2)}) async-start(s8[5898240]{0:T(1024)(128)(4,1)} %bitcast.37), calls=%async_computation.4 | async-start | bytes 8388608
  283.5 50.5 %collective-permute-start.2 = (bf16[320,9216]{1,0:T(8,128)(2,1)}, bf16[320,9216]{1,0:T(8,128)(2,1)}, u32[]{:S(2)}, u32[]{:S(2)}) collective-permute-start(bf16[320,9216]{1,0:T(8,128)(2,1)} %collective-permute-done.1), channel_id=1, source_target_pairs={{0,2},{2,0},{1,3},{3,1},{4,6},{6,4},{5,7},{7,5},{8,10},{10,8},{9,1... | collective-permute-start | bytes 17694728 | tf_op jit(solution)/shard_map/ppermute | solution.py:25
  442.4 46.6 %all-to-all-start.1 = ((bf16[8,2,320,288]{2,3,1,0:T(8,128)(2,1)}), bf16[8,2,320,288]{2,3,1,0:T(8,128)(2,1)}, u32[]{:S(2)}, u32[]{:S(2)}) async-start(bf16[8,2,320,288]{2,3,1,0:T(8,128)(2,1)} %bitcast.40), calls=%async_computation.1 | async-start | bytes 7077888 | tf_op jit(solution)/shard_map/all_to_all | solution.py:61
  494.1 33.6 %copy-start.1 = (bf16[9216,16]{0,1:T(8,128)(2,1)S(1)}, bf16[9216,16]{0,1:T(8,128)(2,1)}, u32[]{:S(2)}) copy-start(bf16[9216,16]{0,1:T(8,128)(2,1)} %param.8) | copy-start | bytes 884740
Sparse Core Ops, SparseCore 0:
  9.6 381.7 all-gather.2
